TPU v7x, 32 devices: a whole 2x2x4 slice. The times are simulated.
32 devices in a mesh: band: 8 (over z, x), sub: 4 (over y, core).
Axes of the slice: x: 2, y: 2, z: 4, core: 2. Of those that a mesh axis runs over, the one named last changes fastest.
Arguments:
- grad_pred: bfloat16 [227, 24576], P(None, ('band', 'sub')), may hold values from -6 to 6
- grid_latent: bfloat16 [24576, 512], P(('band', 'sub')), may hold values from -6 to 6
- mesh_latent: bfloat16 [10240, 512], P(('band', 'sub')), may hold values from -6 to 6
- send_slot: int32 [24576], P(('band', 'sub')), may hold values from 0 to 2303, as said below
- edge_src: int32 [3, 73728], P(None, ('band', 'sub')), may hold values from 0 to 10239, as said below
- w_mesh: bfloat16 [512, 512], replicated, may hold values from -0.25 to 0.25
- w_grid: bfloat16 [512, 512], replicated, may hold values from -0.25 to 0.25
- w_msg: bfloat16 [512, 512], replicated, may hold values from -0.25 to 0.25
- w_out: bfloat16 [512, 227], replicated, may hold values from -0.25 to 0.25
Outputs:
- mesh_grad: bfloat16 [10240, 512], P(('band', 'sub'))
- grad_w_mesh: float32 [512, 512], replicated
- grad_w_grid: float32 [512, 512], replicated
- grad_w_msg: float32 [512, 512], replicated
- grad_w_out: float32 [512, 227], replicated
Inputs may be any that keep to these rules, and one draw needn't show every extreme that they name: For grid point p on latitude-major device i, send_slot[p] = j * 72 + r names patch-major device j and a rank r. On one device i the values are distinct, and for each j the ranks used are 0 to the count of i's points sent to j minus 1. Every such count is at most 72, and 72 is reached in every draw. Every grid point thereby gets one patch-major slot; live slots of each source stand at the front of its block of 72. One patch-major device holds at most 1920 live slots, reached on some device in every draw. `edge_src`: A slot on patch-major device j, of band b = j // 4, names senders in patch b only: mesh rows b * 1280 to (b + 1) * 1280 - 1. Entries of empty slots lie in that range too and are not read.
All inputs are finite; a program needn't handle non-finite values.
Results may differ from a plain program's by a relative error of at most 0.0076.
Values may be sent and summed in bfloat16 or wider, within the bound.
A program may use at most 128 MiB of HBM per device.

v0:
```python
import math

import jax
import jax.numpy as jnp
from jax import lax
from jax.sharding import PartitionSpec as P


def latitude_weight(points, total):
    angle = jnp.pi * ((points.astype(jnp.float32) + 0.5) / total - 0.5)
    return 0.5 * jnp.pi * jnp.cos(angle)


def silu_slope(value):
    sigma = jax.nn.sigmoid(value)
    return sigma * (1.0 + value * (1.0 - sigma))


def contract_rows(left, right):
    return lax.dot_general(
        left, right, (((0,), (0,)), ((), ())), preferred_element_type=jnp.float32
    )


def times_transpose(left, right):
    return lax.dot_general(
        left, right, (((1,), (1,)), ((), ())), preferred_element_type=jnp.float32
    )


def shards(grad_pred, grid_latent, mesh_latent, send_slot, edge_src, w_mesh, w_grid, w_msg, w_out):
    grid_rows = grid_latent.shape[0]
    width = grid_latent.shape[1]
    channels = grad_pred.shape[0]
    devices = lax.axis_size(("band", "sub"))
    capacity = 3 * grid_rows // devices
    total_points = grid_rows * devices
    own_index = lax.axis_index(("band", "sub"))
    points = own_index * grid_rows + jnp.arange(grid_rows, dtype=jnp.int32)
    weighted = (
        latitude_weight(points, total_points)[None, :] * grad_pred.astype(jnp.float32)
    ).astype(jnp.bfloat16)
    target = send_slot // capacity
    slot_rank = send_slot % capacity
    joined = jnp.concatenate([grid_latent, weighted.T], axis=1)
    row_width = width + channels
    send_buffer = (
        jnp.zeros((devices, capacity, row_width), jnp.bfloat16).at[target, slot_rank].set(joined)
    )
    received = lax.all_to_all(send_buffer, ("band", "sub"), split_axis=0, concat_axis=0, tiled=True)
    slots = devices * capacity
    slot_rows = received.reshape(slots, row_width)
    latent_rows = slot_rows[:, :width]
    grad_rows = slot_rows[:, width:]
    grid_proj = jnp.dot(latent_rows, w_grid, preferred_element_type=jnp.float32).astype(
        jnp.bfloat16
    )
    mesh_proj = jnp.dot(mesh_latent, w_mesh, preferred_element_type=jnp.float32).astype(
        jnp.bfloat16
    )
    patch_proj = lax.all_gather(mesh_proj, "sub", axis=0, tiled=True)
    patch_size = patch_proj.shape[0]
    band_index = lax.axis_index("band")
    local_node = edge_src - band_index * patch_size
    grid_float = grid_proj.astype(jnp.float32)
    pre_acts = [
        patch_proj[local_node[corner]].astype(jnp.float32) + grid_float for corner in range(3)
    ]
    act_sum = (
        jax.nn.silu(pre_acts[0]) + jax.nn.silu(pre_acts[1]) + jax.nn.silu(pre_acts[2])
    ).astype(jnp.bfloat16)
    aggregate = jnp.dot(act_sum, w_msg, preferred_element_type=jnp.float32).astype(jnp.bfloat16)
    out_part = contract_rows(aggregate, grad_rows)
    agg_rows = times_transpose(grad_rows, w_out).astype(jnp.bfloat16)
    msg_part = contract_rows(act_sum, agg_rows)
    out_total = lax.psum(out_part, ("band", "sub"))
    msg_total = lax.psum(msg_part, ("band", "sub"))
    act_grad = times_transpose(agg_rows, w_msg)
    pre_grads = [(act_grad * silu_slope(pre)).astype(jnp.bfloat16) for pre in pre_acts]
    grid_proj_grad = (
        pre_grads[0].astype(jnp.float32)
        + pre_grads[1].astype(jnp.float32)
        + pre_grads[2].astype(jnp.float32)
    ).astype(jnp.bfloat16)
    node_part = jnp.zeros((patch_size, width), jnp.float32)
    for corner in range(3):
        node_part = node_part.at[local_node[corner]].add(pre_grads[corner].astype(jnp.float32))
    node_total = lax.psum_scatter(node_part, "sub", scatter_dimension=0, tiled=True)
    grid_part = contract_rows(latent_rows, grid_proj_grad)
    mesh_proj_grad = node_total.astype(jnp.bfloat16)
    mesh_grad = times_transpose(mesh_proj_grad, w_mesh).astype(jnp.bfloat16)
    mesh_part = contract_rows(mesh_latent, mesh_proj_grad)
    grad_scale = 1.0 / math.sqrt(3.0 * total_points)
    grid_total = lax.psum(grid_part, ("band", "sub"))
    mesh_total = lax.psum(mesh_part, ("band", "sub"))
    return (
        mesh_grad,
        mesh_total * grad_scale,
        grid_total * grad_scale,
        msg_total * grad_scale,
        out_total * grad_scale,
    )


def solution(mesh):
    placed = (
        P(None, ("band", "sub")),
        P(("band", "sub"), None),
        P(("band", "sub"), None),
        P(("band", "sub")),
        P(None, ("band", "sub")),
        P(),
        P(),
        P(),
        P(),
    )
    return jax.shard_map(
        shards,
        mesh=mesh,
        in_specs=placed,
        out_specs=(P(("band", "sub"), None), P(), P(), P(), P()),
        check_vma=False,
    )
```

profile of v0, /device:TPU:0, one launch (start us, length us, event | category | flops | bytes accessed | tf_op | source)
XLA Modules:
  0.0 467.3 jit_solution(4389432427457058807)
XLA Ops:
  10.5 2.0 broadcast_in_dim.9
  12.5 101.5 %scatter_fusion = bf16[32,72,739]{2,1,0:T(8,128)(2,1)} fusion(bf16[32,72,739]{2,1,0:T(8,128)(2,1)} %broadcast_in_dim.9, s32[768]{0:T(1024)S(1)} %fusion.23, bf16[768,739]{1,0:T(8,128)(2,1)S(1)} %pad_maximum_fusion), kind=kCustom, calls=%fused_computation.3 | custom fusion | bytes 3411456 | tf_op jit(solution)/shard_map/scatter | solution.py:48
  114.0 7.4 %all-to-all-start = ((bf16[32,72,739]{2,1,0:T(8,128)(2,1)}), bf16[32,72,739]{2,1,0:T(8,128)(2,1)}, u32[]{:S(2)}, u32[]{:S(2)}) async-start(bf16[32,72,739]{2,1,0:T(8,128)(2,1)} %scatter_fusion), calls=%async_computation | async-start | bytes 7077888 | tf_op jit(solution)/shard_map/all_to_all | solution.py:50
  122.8 33.9 %all-gather.2.cloned.1.call-done = bf16[1280,512]{1,0:T(8,128)(2,1)} async-done(((bf16[320,512]{1,0:T(8,128)(2,1)}), bf16[1280,512]{1,0:T(8,128)(2,1)}) %all-gather.2.cloned.1.call-update) | async-done | bytes 1310736 | tf_op jit(solution)/shard_map/all_gather | solution.py:61
  156.7 9.2 %gather_fusion.2 = bf16[2304,512]{1,0:T(8,128)(2,1)} fusion(bf16[1280,512]{1,0:T(8,128)(2,1)} %all-gather.2.cloned.1.call-done, s32[3072]{0:T(1024)S(1)} %get-tuple-element.33), kind=kCustom, calls=%fused_computation.2 | custom fusion | bytes 4727808 | tf_op jit(solution)/shard_map/gather | solution.py:67
  165.9 7.5 %gather_fusion.1 = bf16[2304,512]{1,0:T(8,128)(2,1)} fusion(bf16[1280,512]{1,0:T(8,128)(2,1)S(1)} %copy-done.1, s32[3072]{0:T(1024)S(1)} %get-tuple-element.34), kind=kCustom, calls=%fused_computation.1 | custom fusion | bytes 4727808 | tf_op jit(solution)/shard_map/gather | solution.py:67
  173.5 7.5 %gather_fusion = bf16[2304,512]{1,0:T(8,128)(2,1)} fusion(bf16[1280,512]{1,0:T(8,128)(2,1)S(1)} %copy-done.1, s32[3072]{0:T(1024)S(1)} %pad_clamp_fusion.2), kind=kCustom, calls=%fused_computation | custom fusion | bytes 4727808 | tf_op jit(solution)/shard_map/gather | solution.py:67
  181.0 20.5 %all-to-all-done = bf16[32,72,739]{2,1,0:T(8,128)(2,1)} async-done(((bf16[32,72,739]{2,1,0:T(8,128)(2,1)}), bf16[32,72,739]{2,1,0:T(8,128)(2,1)}, u32[]{:S(2)}, u32[]{:S(2)}) %all-to-all-start) | async-done | bytes 3405344 | tf_op jit(solution)/shard_map/all_to_all | solution.py:50
  201.5 2.0 convolution_convert_fusion.2
  203.6 3.9 convolution_convert_fusion.1
  208.2 9.1 %multiply_convert_fusion = (bf16[2304,512]{1,0:T(8,128)(2,1)}, bf16[2304,512]{1,0:T(8,128)(2,1)}, bf16[2304,512]{1,0:T(8,128)(2,1)}, bf16[2304,512]{1,0:T(8,128)(2,1)}) fusion(bf16[2304,512]{1,0:T(8,128)(2,1)S(1)} %convolution_convert_fusion.1, bf16[2304,512]{1,0:T(8,128)(2,1)S(1)} %copy-done.6, bf16[2304,512]{1,0:T(8,128)(2,1)S(1)} %copy-done.7, ...), kind=kOutput, calls=%fused_computation.20 | convolution fusion | flops 1255145472 | bytes 21757952 | tf_op jit(solution)/shard_map/dot_general | solution.py:26
  217.3 17.0 %scatter_custom_fusion.1 = f32[1280,512]{1,0:T(8,128)S(1)} fusion(s32[2304]{0:T(1024)S(1)} %get-tuple-element.22, bf16[2304,512]{1,0:T(8,128)(2,1)} %get-tuple-element.30, f32[]{:T(128)} %constant.20.clone.1), kind=kCustom, calls=%fused_computation.16 | custom fusion | flops 2359296 | bytes 4980740 | tf_op jit(solution)/shard_map/scatter-add | solution.py:87
  234.3 17.5 %scatter_custom_fusion.2 = f32[1280,512]{1,0:T(8,128)S(1)} fusion(f32[1280,512]{1,0:T(8,128)S(1)} %scatter_custom_fusion.1, s32[2304]{0:T(1024)S(1)} %get-tuple-element.21, bf16[2304,512]{1,0:T(8,128)(2,1)} %get-tuple-element.28), kind=kCustom, calls=%fused_computation.14 | custom fusion | flops 2359296 | bytes 4980736 | tf_op jit(solution)/shard_map/scatter-add | solution.py:87
  251.8 17.4 %scatter_custom_fusion.3 = f32[1280,512]{1,0:T(8,128)S(1)} fusion(f32[1280,512]{1,0:T(8,128)S(1)} %scatter_custom_fusion.2, s32[2304]{0:T(1024)S(1)} %get-tuple-element.20, bf16[2304,512]{1,0:T(8,128)(2,1)} %get-tuple-element.27), kind=kCustom, calls=%fused_computation.11 | custom fusion | flops 2359296 | bytes 4980736 | tf_op jit(solution)/shard_map/scatter-add | solution.py:87
  269.2 1.5 copy-done.2
  271.0 4.8 %fusion.24 = f32[512,512]{0,1:T(8,128)} fusion(bf16[2304,512]{1,0:T(8,128)(2,1)} %get-tuple-element.29, bf16[2304,512]{1,0:T(8,128)(2,1)} %copy-done.5), kind=kOutput, calls=%fused_computation.74 | convolution fusion | flops 1207959552 | bytes 5767168 | tf_op jit(solution)/shard_map/dot_general | solution.py:20
  275.8 5.0 %fusion.12 = f32[512,227]{0,1:T(8,128)} fusion(bf16[2304,739]{1,0:T(8,128)(2,1)} %bitcast.2, bf16[2304,512]{1,0:T(8,128)(2,1)} %get-tuple-element.29, bf16[512,512]{1,0:T(8,128)(2,1)S(1)} %copy-done), kind=kOutput, calls=%fused_computation.37 | convolution fusion | flops 1744699392 | bytes 4528128 | tf_op jit(solution)/shard_map/dot_general | solution.py:20
  280.8 5.5 %fusion.7 = f32[512,512]{0,1:T(8,128)} fusion(bf16[2304,512]{1,0:T(8,128)(2,1)} %get-tuple-element.27, bf16[2304,512]{1,0:T(8,128)(2,1)} %get-tuple-element.28, bf16[2304,512]{1,0:T(8,128)(2,1)S(1)} %copy-done.4, bf16[2304,739]{1,0:T(8,128)(2,1)} %bitcast.2), kind=kOutput, calls=%fused_computation.29 | convolution fusion | flops 1215037440 | bytes 10485760 | tf_op jit(solution)/shard_map/dot_general | solution.py:20
  286.3 19.3 %reduce-scatter.2.cloned.1.call-done = f32[320,512]{1,0:T(8,128)} async-done(((f32[1280,512]{1,0:T(8,128)}), f32[320,512]{1,0:T(8,128)}) %reduce-scatter.2.cloned.1.call-update) | async-done | bytes 655376 | tf_op jit(solution)/shard_map/reduce_scatter | solution.py:88
  305.6 2.6 convolution_bitcast_fusion
  309.3 143.8 %all-reduce.3.cloned.1.call-done = (f32[512,512]{0,1:T(8,128)}, f32[512,512]{0,1:T(8,128)}, f32[512,512]{0,1:T(8,128)}, f32[512,227]{0,1:T(8,128)}) async-done(((f32[512,512]{0,1:T(8,128)}, f32[512,512]{0,1:T(8,128)}, f32[512,512]{0,1:T(8,128)}, f32[512,227]{0,1:T(8,128)}), (f32[512,512]{0,1:T(8,128)}, f32[512,512]{0,1:T(8,128)}, f32[512,512]{0,1:T(8,128)}, ...) | async-done | bytes 3610640 | tf_op jit(solution)/shard_map/psum | solution.py:95
  453.2 1.4 broadcast_multiply_fusion.2
  454.6 1.3 copy.29
  456.7 1.3 broadcast_multiply_fusion.1
  (55 shorter events, 10.2 us)
Async XLA Ops:
  7.2 200.4 %copy-start = (bf16[512,512]{1,0:T(8,128)(2,1)S(1)}, bf16[512,512]{1,0:T(8,128)(2,1)}, u32[]{:S(2)}) copy-start(bf16[512,512]{1,0:T(8,128)(2,1)} %param.16) | copy-start | bytes 1572868
  114.0 7.4 %copy-start.9 = (bf16[512,512]{1,0:T(8,128)(2,1)S(1)}, bf16[512,512]{1,0:T(8,128)(2,1)}, u32[]{:S(2)}) copy-start(bf16[512,512]{1,0:T(8,128)(2,1)} %param.14) | copy-start | bytes 1572868
  114.0 7.4 %copy-start.11 = (bf16[320,512]{1,0:T(8,128)(2,1)S(1)}, bf16[320,512]{1,0:T(8,128)(2,1)}, u32[]{:S(2)}) copy-start(bf16[320,512]{1,0:T(8,128)(2,1)} %param.11) | copy-start | bytes 983044
  114.0 8.6 %copy-start.15 = (s32[3,2304]{1,0:T(4,128)S(1)}, s32[3,2304]{1,0:T(4,128)}, u32[]{:S(2)}) copy-start(s32[3,2304]{1,0:T(4,128)} %param.13) | copy-start | bytes 82948
  114.0 87.4 %all-to-all-start = ((bf16[32,72,739]{2,1,0:T(8,128)(2,1)}), bf16[32,72,739]{2,1,0:T(8,128)(2,1)}, u32[]{:S(2)}, u32[]{:S(2)}) async-start(bf16[32,72,739]{2,1,0:T(8,128)(2,1)} %scatter_fusion), calls=%async_computation | async-start | bytes 7077888 | tf_op jit(solution)/shard_map/all_to_all | solution.py:50
  121.4 35.3 %all-gather.2.cloned.1.call-start = ((), (), s32[]{:S(2)}) async-start(), calls=%async_computation.2 | async-start | bytes 1638400 | tf_op jit(solution)/shard_map/all_gather | solution.py:61
  122.6 183.0 %reduce-scatter.2.cloned.1.call-start = ((), (), s32[]{:S(2)}) async-start(), calls=%async_computation.3 | async-start | bytes 3276800 | tf_op jit(solution)/shard_map/reduce_scatter | solution.py:88
  156.7 9.2 %copy-start.1 = (bf16[1280,512]{1,0:T(8,128)(2,1)S(1)}, bf16[1280,512]{1,0:T(8,128)(2,1)}, u32[]{:S(2)}) copy-start(bf16[1280,512]{1,0:T(8,128)(2,1)} %all-gather.2.cloned.1.call-done) | copy-start | bytes 3932164
  173.5 28.0 %copy-start.14 = (bf16[512,227]{0,1:T(8,128)(2,1)S(1)}, bf16[512,227]{0,1:T(8,128)(2,1)}, u32[]{:S(2)}) copy-start(bf16[512,227]{0,1:T(8,128)(2,1)} %param.17) | copy-start | bytes 697348
  181.0 22.6 %copy-start.16 = (bf16[512,512]{1,0:T(8,128)(2,1)S(1)}, bf16[512,512]{1,0:T(8,128)(2,1)}, u32[]{:S(2)}) copy-start(bf16[512,512]{1,0:T(8,128)(2,1)} %param.15) | copy-start | bytes 1572868
  203.6 4.0 copy-start.5
  203.6 4.0 copy-start.6
  203.6 4.0 copy-start.7
  203.6 4.6 copy-start.8
  269.2 1.5 copy-start.2
  270.7 182.4 %all-reduce.3.cloned.1.call-start = ((), (), s32[]{:S(2)}) async-start(), calls=%async_computation.4 | async-start | bytes 7241728 | tf_op jit(solution)/shard_map/psum | solution.py:95
  275.8 5.0 %copy-start.4 = (bf16[2304,512]{1,0:T(8,128)(2,1)S(1)}, bf16[2304,512]{1,0:T(8,128)(2,1)}, u32[]{:S(2)}) copy-start(bf16[2304,512]{1,0:T(8,128)(2,1)} %get-tuple-element.30) | copy-start | bytes 7077892
  286.3 21.9 %copy-start.10 = (bf16[512,512]{1,0:T(8,128)(2,1)S(1)}, bf16[512,512]{1,0:T(8,128)(2,1)}, u32[]{:S(2)}) copy-start(bf16[512,512]{1,0:T(8,128)(2,1)} %param.14) | copy-start | bytes 1572868
  305.6 2.6 copy-start.3
  453.2 2.7 copy-start.13
  455.9 3.5 copy-start.12
Sparse Core Ops, SparseCore 0:
  124.4 32.3 all-gather.1
  270.9 34.7 reduce-scatter.1
  312.3 140.8 all-reduce.2
where the time goes:
time: 472 us; the launch traced here: 467 us
  waiting for transfers between devices  218 us (46%)
  local copies, waits for them, and re-layouts  134 us (28%)
  other arithmetic  58.8 us (12%)
  matrix products  35.1 us (7%)
  between operations  14 us (3%)
  starting transfers between devices  7.7 us (2%)
    psum x1, waiting for transfers between devices, shards(): mesh_total = lax.psum(mesh_part, ('band', 'sub'))  144 us
    scatter x1, local copies, waits for them, and re-layouts, shards(): jnp.zeros((devices, capacity, row_width), jnp.bfloat16)  102 us
    scatter-add x3, other arithmetic, shards(): node_part.at[local_node[corner]].add(pre_grads[corner].astype(jnp.float32))  51.9 us
    all_gather x1, waiting for transfers between devices, shards(): patch_proj = lax.all_gather(mesh_proj, 'sub', axis=0, tiled=True)  33.9 us
    gather x3, local copies, waits for them, and re-layouts, shards(): patch_proj[local_node[corner]].astype(jnp.float32) + grid_float  24.2 us
    all_to_all x1, waiting for transfers between devices, shards(): lax.all_to_all(send_buffer, ('band', 'sub'), split_axis=0, concat_axis=0,...  20.5 us
    reduce_scatter x1, waiting for transfers between devices, shards(): lax.psum_scatter(node_part, 'sub', scatter_dimension=0, tiled=True)  19.3 us
    dot_general x4, matrix products, contract_rows(): lax.dot_general(left, right, (((0,), (0,)), ((), ())), preferred_element_...  17.9 us
  transfers between devices with their start and end apart: 4, of which 4 were waited for; matrix products, arithmetic and copies ran while one was open for 9% of the time, Pallas kernels for 0%

commit v1 on v0

v1 whole, which is shorter than its diff:
```python
import math

import jax
import jax.numpy as jnp
from jax import lax
from jax.sharding import PartitionSpec as P


def latitude_weight(points, total):
    angle = jnp.pi * ((points.astype(jnp.float32) + 0.5) / total - 0.5)
    return 0.5 * jnp.pi * jnp.cos(angle)


def silu_slope(value):
    sigma = jax.nn.sigmoid(value)
    return sigma * (1.0 + value * (1.0 - sigma))


def contract_rows(left, right):
    return lax.dot_general(
        left, right, (((0,), (0,)), ((), ())), preferred_element_type=jnp.float32
    )


def times_transpose(left, right):
    return lax.dot_general(
        left, right, (((1,), (1,)), ((), ())), preferred_element_type=jnp.float32
    )


def spread(rows, index, slots):
    places = lax.broadcasted_iota(jnp.int32, (slots, index.shape[0]), 0)
    return (places == index[None, :]).astype(rows.dtype)


def shards(grad_pred, grid_latent, mesh_latent, send_slot, edge_src, w_mesh, w_grid, w_msg, w_out):
    both = ("band", "sub")
    grid_rows, width = grid_latent.shape
    channels = grad_pred.shape[0]
    devices = lax.axis_size(both)
    subs = lax.axis_size("sub")
    capacity = 3 * grid_rows // devices
    total_points = grid_rows * devices
    slots = devices * capacity
    own_index = lax.axis_index(both)
    points = own_index * grid_rows + jnp.arange(grid_rows, dtype=jnp.int32)
    weighted = (
        latitude_weight(points, total_points)[None, :] * grad_pred.astype(jnp.float32)
    ).astype(jnp.bfloat16)
    one_hot = spread(grid_latent, send_slot, slots)
    latent_send = jnp.dot(one_hot, grid_latent, preferred_element_type=jnp.float32).astype(
        jnp.bfloat16
    )
    grad_send = times_transpose(one_hot, weighted).astype(jnp.bfloat16)
    latent_rows = lax.all_to_all(
        latent_send.reshape(devices, capacity, width), both, split_axis=0, concat_axis=0, tiled=True
    ).reshape(slots, width)
    grad_rows = lax.all_to_all(
        grad_send.reshape(devices, capacity, channels), both, split_axis=0, concat_axis=0, tiled=True
    ).reshape(slots, channels)
    patch_latent = lax.all_gather(mesh_latent, "sub", axis=0, tiled=True)
    patch_size = patch_latent.shape[0]
    patch_proj = jnp.dot(patch_latent, w_mesh, preferred_element_type=jnp.float32).astype(
        jnp.bfloat16
    )
    local_node = edge_src - lax.axis_index("band") * patch_size
    nodes = lax.broadcasted_iota(jnp.int32, (slots, patch_size), 1)
    grid_float = (
        jnp.dot(latent_rows, w_grid, preferred_element_type=jnp.float32)
        .astype(jnp.bfloat16)
        .astype(jnp.float32)
    )
    pre_acts = [
        jnp.dot(
            (nodes == local_node[corner][:, None]).astype(jnp.bfloat16),
            patch_proj,
            preferred_element_type=jnp.float32,
        )
        + grid_float
        for corner in range(3)
    ]
    act_sum = (
        jax.nn.silu(pre_acts[0]) + jax.nn.silu(pre_acts[1]) + jax.nn.silu(pre_acts[2])
    ).astype(jnp.bfloat16)
    aggregate = jnp.dot(act_sum, w_msg, preferred_element_type=jnp.float32).astype(jnp.bfloat16)
    out_part = contract_rows(aggregate, grad_rows)
    agg_rows = times_transpose(grad_rows, w_out).astype(jnp.bfloat16)
    msg_part = contract_rows(act_sum, agg_rows)
    act_grad = times_transpose(agg_rows, w_msg)
    pre_grads = [(act_grad * silu_slope(pre)).astype(jnp.bfloat16) for pre in pre_acts]
    grid_proj_grad = (
        pre_grads[0].astype(jnp.float32)
        + pre_grads[1].astype(jnp.float32)
        + pre_grads[2].astype(jnp.float32)
    ).astype(jnp.bfloat16)
    targets = lax.broadcasted_iota(jnp.int32, (patch_size, slots), 0)
    node_part = sum(
        jnp.dot(
            (targets == local_node[corner][None, :]).astype(jnp.bfloat16),
            pre_grads[corner],
            preferred_element_type=jnp.float32,
        )
        for corner in range(3)
    ).astype(jnp.bfloat16)
    node_parts = lax.all_to_all(
        node_part.reshape(subs, patch_size // subs, width),
        "sub",
        split_axis=0,
        concat_axis=0,
        tiled=True,
    )
    grid_part = contract_rows(latent_rows, grid_proj_grad)
    mesh_part = contract_rows(patch_latent, node_part)
    parts = jnp.concatenate([mesh_part, grid_part, msg_part, out_part], axis=1).astype(jnp.bfloat16)
    exchanged = lax.all_to_all(
        parts.reshape(devices, width // devices, parts.shape[1]),
        both,
        split_axis=0,
        concat_axis=0,
        tiled=True,
    )
    own_rows = jnp.sum(exchanged.astype(jnp.float32), axis=0).astype(jnp.bfloat16)
    totals = lax.all_gather(own_rows, both, axis=0, tiled=True)
    mesh_proj_grad = jnp.sum(node_parts.astype(jnp.float32), axis=0).astype(jnp.bfloat16)
    mesh_grad = times_transpose(mesh_proj_grad, w_mesh).astype(jnp.bfloat16)
    grad_scale = 1.0 / math.sqrt(3.0 * total_points)
    scaled = totals.astype(jnp.float32) * grad_scale
    return (
        mesh_grad,
        scaled[:, :width],
        scaled[:, width : 2 * width],
        scaled[:, 2 * width : 3 * width],
        scaled[:, 3 * width :],
    )


def solution(mesh):
    placed = (
        P(None, ("band", "sub")),
        P(("band", "sub"), None),
        P(("band", "sub"), None),
        P(("band", "sub")),
        P(None, ("band", "sub")),
        P(),
        P(),
        P(),
        P(),
    )
    return jax.shard_map(
        shards,
        mesh=mesh,
        in_specs=placed,
        out_specs=(P(("band", "sub"), None), P(), P(), P(), P()),
        check_vma=False,
    )
```

time: 472 us -> 263 us (0.56)
  local copies, waits for them, and re-layouts: 134 us -> 10.3 us
  waiting for transfers between devices: 218 us -> 103 us
  blocking collectives: 0 us -> 67.4 us
  other arithmetic: 58.8 us -> 3.27 us
  matrix products: 35.1 us -> 53.3 us
    psum x1 -> x0, waiting for transfers between devices: 144 us -> none  [shards(): mesh_total = lax.psum(mesh_part, ('band', 'sub'))]
    scatter x1 -> x0, local copies, waits for them, and re-layouts: 102 us -> none  [shards(): jnp.zeros((devices, capacity, row_width), jnp.bfloat16)]
    all_to_all x0 -> x2, blocking collectives: none -> 67.4 us  [the longest x1 47.1 us: shards(): lax.all_to_all(parts.reshape(devices, width // devices, parts.shape[1]),...]
    scatter-add x3 -> x0, other arithmetic: 51.9 us -> none  [shards(): node_part.at[local_node[corner]].add(pre_grads[corner].astype(jnp.float32))]
    dot_general x1 -> x9, matrix products: 1.06 us -> 35.3 us  [the longest x3 17.1 us: shards(): jnp.dot((nodes == local_node[corner][:, None]).astype(jnp.bfloat16), patc...]
    all_gather x1 -> x2, waiting for transfers between devices: 33.9 us -> 63.4 us  [the longest x1 32.3 us: shards(): totals = lax.all_gather(own_rows, both, axis=0, tiled=True)]
    gather x3 -> x0, local copies, waits for them, and re-layouts: 24.2 us -> none  [shards(): patch_proj[local_node[corner]].astype(jnp.float32) + grid_float]
    reduce_scatter x1 -> x0, waiting for transfers between devices: 19.3 us -> none  [shards(): lax.psum_scatter(node_part, 'sub', scatter_dimension=0, tiled=True)]
  transfers between devices with their start and end apart: 4 -> 4, of which waited for: 4 -> 4; matrix products, arithmetic and copies ran while one was open for 9% -> 6% of each run, Pallas kernels for 0% -> 0%
where the time goes in v1:
time: 263 us
  waiting for transfers between devices  103 us (39%)
  blocking collectives  67.4 us (26%)
  matrix products  53.3 us (20%)
  between operations  14.4 us (5%)
  starting transfers between devices  11.2 us (4%)
  local copies, waits for them, and re-layouts  10.3 us (4%)
  other arithmetic  3.27 us (1%)
    all_to_all x1, blocking collectives, shards(): lax.all_to_all(parts.reshape(devices, width // devices, parts.shape[1]),...  47.1 us
    all_gather x1, waiting for transfers between devices, shards(): totals = lax.all_gather(own_rows, both, axis=0, tiled=True)  32.3 us
    all_gather x1, waiting for transfers between devices, shards(): patch_latent = lax.all_gather(mesh_latent, 'sub', axis=0, tiled=True)  31.1 us
    all_to_all x1, waiting for transfers between devices, shards(): lax.all_to_all(grad_send.reshape(devices, capacity, channels), both, spli...  25.5 us
    all_to_all x1, blocking collectives, shards(): lax.all_to_all(node_part.reshape(subs, patch_size // subs, width), 'sub',...  20.2 us
    dot_general x3, matrix products, shards(): jnp.dot((nodes == local_node[corner][:, None]).astype(jnp.bfloat16), patc...  17.1 us
    all_to_all x1, waiting for transfers between devices, shards(): lax.all_to_all(latent_send.reshape(devices, capacity, width), both, split...  13.2 us
    dot_general x4, matrix products, times_transpose(): lax.dot_general(left, right, (((1,), (1,)), ((), ())), preferred_element_...  10.2 us
  transfers between devices with their start and end apart: 4, of which 4 were waited for; matrix products, arithmetic and copies ran while one was open for 6% of the time, Pallas kernels for 0%

profile of v1, /device:TPU:0, one launch (start us, length us, event | category | flops | bytes accessed | tf_op | source)
XLA Modules:
  0.0 262.6 jit_solution(13357038231698824448)
XLA Ops:
  7.2 2.7 %fusion.15 = bf16[2304,227]{0,1:T(8,128)(2,1)S(1)} fusion(s32[768]{0:T(1024)} %param.12, bf16[227,768]{1,0:T(8,128)(2,1)} %param.9, f32[768]{0:T(1024)S(1)} %cosine_multiply_fusion), kind=kOutput, calls=%fused_computation.36 | convolution fusion | flops 806155776 | bytes 1400832 | tf_op jit(solution)/shard_map/dot_general | solution.py:26
  11.4 7.3 %all-to-all-start = ((bf16[32,72,227]{2,1,0:T(8,128)(2,1)}), bf16[32,72,227]{2,1,0:T(8,128)(2,1)S(1)}, u32[]{:S(2)}, u32[]{:S(2)}) async-start(bf16[32,72,227]{2,1,0:T(8,128)(2,1)} %bitcast), calls=%async_computation | async-start | bytes 2359296 | tf_op jit(solution)/shard_map/all_to_all | solution.py:58
  18.8 3.5 %fusion.14 = bf16[2304,512]{1,0:T(8,128)(2,1)} fusion(bf16[768,512]{1,0:T(8,128)(2,1)S(1)} %copy-done, s32[768]{0:T(1024)S(1)} %copy-done.12), kind=kOutput, calls=%fused_computation.32 | convolution fusion | flops 1814888448 | bytes 3148800 | tf_op jit(solution)/shard_map/dot_general | solution.py:51
  22.3 25.5 %all-to-all-done = bf16[32,72,227]{2,1,0:T(8,128)(2,1)S(1)} async-done(((bf16[32,72,227]{2,1,0:T(8,128)(2,1)}), bf16[32,72,227]{2,1,0:T(8,128)(2,1)S(1)}, u32[]{:S(2)}, u32[]{:S(2)}) %all-to-all-start) | async-done | bytes 1046048 | tf_op jit(solution)/shard_map/all_to_all | solution.py:58
  47.8 3.7 %all-to-all-start.1 = ((bf16[32,72,512]{2,1,0:T(8,128)(2,1)}), bf16[32,72,512]{2,1,0:T(8,128)(2,1)}, u32[]{:S(2)}, u32[]{:S(2)}) async-start(bf16[32,72,512]{2,1,0:T(8,128)(2,1)} %bitcast.52), calls=%async_computation.1 | async-start | bytes 4718592 | tf_op jit(solution)/shard_map/all_to_all | solution.py:55
  53.0 31.1 %all-gather.3.cloned.1.call-done = bf16[1280,512]{1,0:T(8,128)(2,1)} async-done(((bf16[320,512]{1,0:T(8,128)(2,1)}), bf16[1280,512]{1,0:T(8,128)(2,1)}) %all-gather.3.cloned.1.call-update) | async-done | bytes 1310736 | tf_op jit(solution)/shard_map/all_gather | solution.py:61
  84.1 3.2 %convolution_convert_fusion.3 = bf16[1280,512]{1,0:T(8,128)(2,1)} fusion(bf16[1280,512]{1,0:T(8,128)(2,1)} %all-gather.3.cloned.1.call-done, bf16[512,512]{1,0:T(8,128)(2,1)S(1)} %copy-done.7), kind=kOutput, calls=%fused_computation.42 | convolution fusion | flops 671744000 | bytes 3145728 | tf_op jit(solution)/shard_map/dot_general | solution.py:63
  87.3 1.8 convolution_convert_fusion.2
  89.1 3.6 %fusion.29 = f32[2304,512]{1,0:T(8,128)} fusion(bf16[2304,512]{1,0:T(8,128)(2,1)S(1)} %convolution_convert_fusion.2, bf16[512,512]{1,0:T(8,128)(2,1)S(1)} %copy-done.5), kind=kOutput, calls=%fused_computation.60 | convolution fusion | flops 1207959552 | bytes 7602176 | tf_op jit(solution)/shard_map/dot_general | solution.py:26
  92.6 13.2 %all-to-all-done.1 = bf16[32,72,512]{2,1,0:T(8,128)(2,1)} async-done(((bf16[32,72,512]{2,1,0:T(8,128)(2,1)}), bf16[32,72,512]{2,1,0:T(8,128)(2,1)}, u32[]{:S(2)}, u32[]{:S(2)}) %all-to-all-start.1) | async-done | bytes 2359328 | tf_op jit(solution)/shard_map/all_to_all | solution.py:55
  105.9 4.3 %copy.25 = bf16[2304,512]{0,1:T(8,128)(2,1)} copy(bf16[2304,512]{1,0:T(8,128)(2,1)} %bitcast.3) | data formatting | bytes 4718592 | tf_op jit(solution)/shard_map/reshape | solution.py:57
  110.2 3.2 %convolution_convert_fusion.1 = bf16[2304,512]{1,0:T(8,128)(2,1)S(1)} fusion(bf16[2304,512]{1,0:T(8,128)(2,1)} %bitcast.3, bf16[512,512]{1,0:T(8,128)(2,1)} %param.15), kind=kOutput, calls=%fused_computation.34 | convolution fusion | flops 1209139200 | bytes 5242880 | tf_op jit(solution)/shard_map/dot_general | solution.py:69
  113.5 3.5 %convert_add_fusion.1 = f32[2304,512]{1,0:T(8,128)S(1)} fusion(bf16[2304,512]{1,0:T(8,128)(2,1)S(1)} %convolution_convert_fusion.1, bf16[1280,512]{1,0:T(8,128)(2,1)S(1)} %copy-done.13, s32[2304]{0:T(1024)S(1)} %copy-done.9), kind=kOutput, calls=%fused_computation.16 | convolution fusion | flops 3025207296 | bytes 8397824 | tf_op jit(solution)/shard_map/dot_general | solution.py:74
  117.0 3.5 %convert_add_fusion.2 = f32[2304,512]{1,0:T(8,128)S(1)} fusion(bf16[2304,512]{1,0:T(8,128)(2,1)S(1)} %convolution_convert_fusion.1, bf16[1280,512]{1,0:T(8,128)(2,1)S(1)} %copy-done.13, s32[2304]{0:T(1024)S(1)} %copy-done.10), kind=kOutput, calls=%fused_computation.17 | convolution fusion | flops 3025207296 | bytes 8397824 | tf_op jit(solution)/shard_map/dot_general | solution.py:74
  120.6 10.1 %add_convert_fusion = (bf16[2304,512]{1,0:T(8,128)(2,1)S(1)}, bf16[2304,512]{1,0:T(8,128)(2,1)S(1)}, bf16[2304,512]{1,0:T(8,128)(2,1)S(1)}, bf16[2304,512]{1,0:T(8,128)(2,1)S(1)}) fusion(f32[2304,512]{1,0:T(8,128)S(1)} %convert_add_fusion.1, f32[2304,512]{1,0:T(8,128)S(1)} %convert_add_fusion.2, f32[2304,512]{1,0:T(8,128)S(1)} %bitcast.49, ...), kind=kOutput, calls=%fused_computation.24 | convolution fusion | flops 3064135680 | bytes 27272192 | tf_op jit(solution)/shard_map/dot_general | solution.py:74
  133.6 3.2 %fusion = f32[1280,512]{1,0:T(8,128)S(1)} fusion(bf16[2304,512]{1,0:T(8,128)(2,1)S(1)} %get-tuple-element.24, s32[2304]{0:T(1024)S(1)} %copy-done.10), kind=kOutput, calls=%fused_computation.6 | convolution fusion | flops 3022848000 | bytes 4989952 | tf_op jit(solution)/shard_map/dot_general | solution.py:98
  136.8 3.2 %fusion.19 = f32[1280,512]{1,0:T(8,128)S(1)} fusion(f32[1280,512]{1,0:T(8,128)S(1)} %fusion, bf16[2304,512]{1,0:T(8,128)(2,1)S(1)} %get-tuple-element.25, s32[2304]{0:T(1024)S(1)} %copy-done.9), kind=kOutput, calls=%fused_computation.41 | convolution fusion | flops 3023503360 | bytes 7611392 | tf_op jit(solution)/shard_map/dot_general | solution.py:98
  141.5 3.6 %fusion.20 = bf16[1280,512]{1,0:T(8,128)(2,1)S(1)} fusion(f32[1280,512]{1,0:T(8,128)S(1)} %fusion.19, bf16[2304,512]{1,0:T(8,128)(2,1)S(1)} %get-tuple-element.26, s32[2304]{0:T(1024)S(1)} %get-tuple-element.20), kind=kOutput, calls=%fused_computation.43 | convolution fusion | flops 3024158720 | bytes 6300672 | tf_op jit(solution)/shard_map/dot_general | solution.py:98
  148.0 47.1 %all_to_all.20 = bf16[32,16,1763]{2,1,0:T(8,128)(2,1)S(1)} all-to-all(bf16[32,16,1763]{2,1,0:T(8,128)(2,1)S(1)} %pad_maximum_fusion), channel_id=1, replica_groups=mesh['band'=8,'sub'=4] {'band','sub'}, dimensions={0} | all-to-all | bytes 3610624 | tf_op jit(solution)/shard_map/all_to_all | solution.py:115
  196.1 20.2 %all_to_all.21 = bf16[4,320,512]{2,1,0:T(8,128)(2,1)S(1)} all-to-all(bf16[4,320,512]{2,1,0:T(8,128)(2,1)S(1)} %bitcast.54), channel_id=1, replica_groups=mesh['band'=8,'sub'=4] {'sub'}, dimensions={0} | all-to-all | bytes 2621440 | tf_op jit(solution)/shard_map/all_to_all | solution.py:105
  216.7 2.1 convolution_convert_fusion.6
  218.8 32.3 %all-gather.5.cloned.1.call-done = bf16[512,1763]{1,0:T(8,128)(2,1)} async-done(((bf16[16,1763]{1,0:T(8,128)(2,1)}), bf16[512,1763]{1,0:T(8,128)(2,1)}) %all-gather.5.cloned.1.call-update) | async-done | bytes 1805328 | tf_op jit(solution)/shard_map/all_gather | solution.py:123
  251.1 1.8 convert_multiply_fusion
  252.9 1.8 fusion.28
  (51 shorter events, 12.5 us)
Async XLA Ops:
  7.2 11.6 %copy-start = (bf16[768,512]{1,0:T(8,128)(2,1)S(1)}, bf16[768,512]{1,0:T(8,128)(2,1)}, u32[]{:S(2)}) copy-start(bf16[768,512]{1,0:T(8,128)(2,1)} %param.10) | copy-start | bytes 2359300
  10.0 8.8 %copy-start.12 = (s32[768]{0:T(1024)S(1)}, s32[768]{0:T(1024)}, u32[]{:S(2)}) copy-start(s32[768]{0:T(1024)} %param.12) | copy-start | bytes 9220
  11.4 36.4 %all-to-all-start = ((bf16[32,72,227]{2,1,0:T(8,128)(2,1)}), bf16[32,72,227]{2,1,0:T(8,128)(2,1)S(1)}, u32[]{:S(2)}, u32[]{:S(2)}) async-start(bf16[32,72,227]{2,1,0:T(8,128)(2,1)} %bitcast), calls=%async_computation | async-start | bytes 2359296 | tf_op jit(solution)/shard_map/all_to_all | solution.py:58
  22.3 30.0 %copy-start.8 = (s32[3,2304]{1,0:T(4,128)S(1)}, s32[3,2304]{1,0:T(4,128)}, u32[]{:S(2)}) copy-start(s32[3,2304]{1,0:T(4,128)} %param.13) | copy-start | bytes 82948
  22.3 61.8 %copy-start.7 = (bf16[512,512]{1,0:T(8,128)(2,1)S(1)}, bf16[512,512]{1,0:T(8,128)(2,1)}, u32[]{:S(2)}) copy-start(bf16[512,512]{1,0:T(8,128)(2,1)} %param.14) | copy-start | bytes 1572868
  47.8 58.1 %all-to-all-start.1 = ((bf16[32,72,512]{2,1,0:T(8,128)(2,1)}), bf16[32,72,512]{2,1,0:T(8,128)(2,1)}, u32[]{:S(2)}, u32[]{:S(2)}) async-start(bf16[32,72,512]{2,1,0:T(8,128)(2,1)} %bitcast.52), calls=%async_computation.1 | async-start | bytes 4718592 | tf_op jit(solution)/shard_map/all_to_all | solution.py:55
  51.5 32.6 %all-gather.3.cloned.1.call-start = ((), (), s32[]{:S(2)}) async-start(), calls=%async_computation.4 | async-start | bytes 1638400 | tf_op jit(solution)/shard_map/all_gather | solution.py:61
  52.3 198.8 %all-gather.5.cloned.1.call-start = ((), (), s32[]{:S(2)}) async-start(), calls=%async_computation.5 | async-start | bytes 1892352 | tf_op jit(solution)/shard_map/all_gather | solution.py:123
  87.3 1.8 copy-start.5
  110.2 3.2 %copy-start.9 = (s32[2304]{0:T(1024)S(1)}, s32[2304]{0:T(1024)}, u32[]{:S(2)}) copy-start(s32[2304]{0:T(1024)} %get-tuple-element.21) | copy-start | bytes 27652
  110.2 3.3 %copy-start.13 = (bf16[1280,512]{1,0:T(8,128)(2,1)S(1)}, bf16[1280,512]{1,0:T(8,128)(2,1)}, u32[]{:S(2)}) copy-start(bf16[1280,512]{1,0:T(8,128)(2,1)} %convolution_convert_fusion.3) | copy-start | bytes 3932164
  113.4 3.6 %copy-start.10 = (s32[2304]{0:T(1024)S(1)}, s32[2304]{0:T(1024)}, u32[]{:S(2)}) copy-start(s32[2304]{0:T(1024)} %get-tuple-element.22) | copy-start | bytes 27652
  113.4 7.1 %slice-start = ((s8[4718592]{0:T(1024)(128)(4,1)}), s8[4194304]{0:T(1024)(128)(4,1)S(1)}, s32[]{:S(2)}) async-start(s8[4718592]{0:T(1024)(128)(4,1)} %bitcast.48), calls=%async_computation.6 | async-start | bytes 8388608
  117.0 3.6 %slice-start.1 = ((s8[4718592]{0:T(1024)(128)(4,1)}), s8[524288]{0:T(1024)(128)(4,1)S(1)}, s32[]{:S(2)}) async-start(s8[4718592]{0:T(1024)(128)(4,1)} %bitcast.48), calls=%async_computation.7 | async-start | bytes 1048576
  130.6 1.4 copy-start.6
  136.8 3.3 %copy-start.2 = (bf16[2304,512]{0,1:T(8,128)(2,1)S(1)}, bf16[2304,512]{0,1:T(8,128)(2,1)}, u32[]{:S(2)}) copy-start(bf16[2304,512]{0,1:T(8,128)(2,1)} %copy.25) | copy-start | bytes 7077892
  145.1 2.7 %copy-start.3 = (bf16[1280,512]{1,0:T(8,128)(2,1)}, bf16[1280,512]{1,0:T(8,128)(2,1)S(1)}, u32[]{:S(2)}) copy-start(bf16[1280,512]{1,0:T(8,128)(2,1)S(1)} %fusion.20) | copy-start | bytes 3932164
  145.1 1.8 copy-start.11
  148.0 48.1 %copy-start.4 = (bf16[1280,512]{1,0:T(8,128)(2,1)S(1)}, bf16[1280,512]{1,0:T(8,128)(2,1)}, u32[]{:S(2)}) copy-start(bf16[1280,512]{1,0:T(8,128)(2,1)} %copy-done.3) | copy-start | bytes 3932164
  252.9 2.8 %copy-start.1 = (bf16[768,512]{1,0:T(8,128)(2,1)S(1)}, bf16[768,512]{1,0:T(8,128)(2,1)}, u32[]{:S(2)}) copy-start(bf16[768,512]{1,0:T(8,128)(2,1)} %param.10) | copy-start | bytes 2359300
Sparse Core Ops, SparseCore 0:
  53.9 30.1 all-gather.2
  196.2 54.8 all-gather.4

commit v2 on v1

--- a/solution.py
+++ b/solution.py
@@ -1,8 +1,11 @@
+import functools
 import math
 
 import jax
 import jax.numpy as jnp
 from jax import lax
+from jax.experimental import pallas as pl
+from jax.experimental.pallas import tpu as pltpu
 from jax.sharding import PartitionSpec as P
 
 
@@ -31,6 +34,209 @@
 def spread(rows, index, slots):
     places = lax.broadcasted_iota(jnp.int32, (slots, index.shape[0]), 0)
     return (places == index[None, :]).astype(rows.dtype)
+
+
+def reduce_kernel(
+    subs,
+    parts_ref,
+    nodes_ref,
+    total_ref,
+    node_ref,
+    half_in,
+    half_sum,
+    group_in,
+    node_in,
+    node_sum,
+    node_last,
+    half_sem,
+    group_send,
+    group_recv,
+    own_send,
+    own_recv,
+    pass_send,
+    pass_recv,
+    node_send,
+    node_recv,
+    last_send,
+    last_recv,
+):
+    devices = parts_ref.shape[0]
+    groups = devices // 2
+    sub_groups = subs // 2
+    band, sub = lax.axis_index("band"), lax.axis_index("sub")
+    me = band * subs + sub
+    parity, group = me % 2, me // 2
+    other = 1 - parity
+    partner = me + 1 - 2 * parity
+    own_pair = sub // 2
+
+    def remote(src, dst, send_sem, recv_sem, device):
+        return pltpu.make_async_remote_copy(
+            src_ref=src,
+            dst_ref=dst,
+            send_sem=send_sem,
+            recv_sem=recv_sem,
+            device_id=(device // subs, device % subs),
+            device_id_type=pl.DeviceIdType.MESH,
+        )
+
+    def member(index):
+        return 2 * index + parity
+
+    def ahead(step):
+        return (group + step) % groups
+
+    def behind(step):
+        return (group + groups - step) % groups
+
+    barrier = pltpu.get_barrier_semaphore()
+
+    def greet(device):
+        pl.semaphore_signal(
+            barrier,
+            inc=1,
+            device_id=(device // subs, device % subs),
+            device_id_type=pl.DeviceIdType.MESH,
+        )
+
+    greet(partner)
+
+    @pl.loop(1, groups)
+    def _(step):
+        greet(member(ahead(step)))
+
+    pl.semaphore_wait(barrier, groups)
+
+    half_copy = remote(
+        parts_ref.at[pl.ds(other * groups, groups)], half_in, half_sem.at[0], half_sem.at[1], partner
+    )
+    half_copy.start()
+    node_copies = [
+        remote(
+            nodes_ref.at[2 * pair + other],
+            node_in.at[pair],
+            node_send.at[pair],
+            node_recv.at[pair],
+            partner,
+        )
+        for pair in range(sub_groups)
+    ]
+    for copy in node_copies:
+        copy.start()
+    half_copy.wait()
+
+    def add_half(index):
+        return parts_ref[parity * groups + index].astype(jnp.float32) + half_in[index].astype(
+            jnp.float32
+        )
+
+    def group_copy(source, target):
+        return remote(
+            half_sum.at[target],
+            group_in.at[source],
+            group_send.at[target],
+            group_recv.at[source],
+            member(target),
+        )
+
+    @pl.loop(1, groups)
+    def _(step):
+        target = ahead(step)
+        half_sum[target] = add_half(target).astype(half_sum.dtype)
+        group_copy(group, target).start()
+
+    for copy in node_copies:
+        copy.wait()
+
+    def last_copy(source, target):
+        return remote(
+            node_sum.at[target],
+            node_last.at[source],
+            last_send.at[target],
+            last_recv.at[source],
+            band * subs + 2 * target + parity,
+        )
+
+    def add_node(pair):
+        return nodes_ref[2 * pair + parity].astype(jnp.float32) + node_in[pair].astype(jnp.float32)
+
+    for step in range(1, sub_groups):
+        target = (own_pair + step) % sub_groups
+        node_sum[target] = add_node(target).astype(node_sum.dtype)
+        last_copy(own_pair, target).start()
+
+    def take(step, running):
+        source = behind(step)
+        group_copy(source, source).wait_recv()
+        return running + group_in[source].astype(jnp.float32)
+
+    mine = parity * groups + group
+    total_ref[mine] = lax.fori_loop(1, groups, take, add_half(group)).astype(total_ref.dtype)
+
+    def own_copy(source, target):
+        place = total_ref.at[parity * groups + source]
+        return remote(place, place, own_send.at[target], own_recv.at[source], member(target))
+
+    def pass_copy(source, half):
+        place = total_ref.at[half * groups + source]
+        return remote(place, place, pass_send.at[source], pass_recv.at[source], partner)
+
+    @pl.loop(1, groups)
+    def _(step):
+        own_copy(group, ahead(step)).start()
+
+    pass_copy(group, parity).start()
+
+    running = add_node(own_pair)
+    for step in range(1, sub_groups):
+        source = (own_pair + sub_groups - step) % sub_groups
+        last_copy(source, source).wait_recv()
+        running = running + node_last[source].astype(jnp.float32)
+    node_ref[...] = running.astype(node_ref.dtype)
+
+    @pl.loop(1, groups)
+    def _(step):
+        source = behind(step)
+        own_copy(source, source).wait_recv()
+        pass_copy(source, parity).start()
+
+    @pl.loop(0, groups)
+    def _(step):
+        source = ahead(step)
+        pass_copy(source, other).wait_recv()
+        pass_copy(source, parity).wait_send()
+
+    @pl.loop(1, groups)
+    def _(step):
+        target = ahead(step)
+        group_copy(group, target).wait_send()
+        own_copy(group, target).wait_send()
+
+    for step in range(1, sub_groups):
+        last_copy(own_pair, (own_pair + step) % sub_groups).wait_send()
+
+
+def reduce_all(parts, nodes):
+    devices, rows, columns = parts.shape
+    subs, node_rows, width = nodes.shape
+    groups, sub_groups = devices // 2, subs // 2
+    vmem = pl.BlockSpec(memory_space=pltpu.VMEM)
+    dma = pltpu.SemaphoreType.DMA
+    return pl.pallas_call(
+        functools.partial(reduce_kernel, subs),
+        out_shape=(
+            jax.ShapeDtypeStruct(parts.shape, parts.dtype),
+            jax.ShapeDtypeStruct((node_rows, width), nodes.dtype),
+        ),
+        in_specs=[vmem, vmem],
+        out_specs=(vmem, vmem),
+        scratch_shapes=[pltpu.VMEM((groups, rows, columns), parts.dtype)] * 3
+        + [pltpu.VMEM((sub_groups, node_rows, width), nodes.dtype)] * 3
+        + [dma((2,))]
+        + [dma((groups,))] * 6
+        + [dma((sub_groups,))] * 4,
+        compiler_params=pltpu.CompilerParams(collective_id=0, has_side_effects=True),
+    )(parts, nodes)
 
 
 def shards(grad_pred, grid_latent, mesh_latent, send_slot, edge_src, w_mesh, w_grid, w_msg, w_out):
@@ -47,18 +253,29 @@
     weighted = (
         latitude_weight(points, total_points)[None, :] * grad_pred.astype(jnp.float32)
     ).astype(jnp.bfloat16)
+    padding = -channels % 128
+    weighted = jnp.pad(weighted, ((0, padding), (0, 0)))
+    w_out = jnp.pad(w_out, ((0, 0), (0, padding)))
+    patch_latent = lax.all_gather(mesh_latent, "sub", axis=0, tiled=True)
     one_hot = spread(grid_latent, send_slot, slots)
     latent_send = jnp.dot(one_hot, grid_latent, preferred_element_type=jnp.float32).astype(
         jnp.bfloat16
     )
     grad_send = times_transpose(one_hot, weighted).astype(jnp.bfloat16)
     latent_rows = lax.all_to_all(
-        latent_send.reshape(devices, capacity, width), both, split_axis=0, concat_axis=0, tiled=True
+        latent_send.reshape(devices, capacity, width),
+        both,
+        split_axis=0,
+        concat_axis=0,
+        tiled=True,
     ).reshape(slots, width)
     grad_rows = lax.all_to_all(
-        grad_send.reshape(devices, capacity, channels), both, split_axis=0, concat_axis=0, tiled=True
-    ).reshape(slots, channels)
-    patch_latent = lax.all_gather(mesh_latent, "sub", axis=0, tiled=True)
+        grad_send.reshape(devices, capacity, channels + padding),
+        both,
+        split_axis=0,
+        concat_axis=0,
+        tiled=True,
+    ).reshape(slots, channels + padding)
     patch_size = patch_latent.shape[0]
     patch_proj = jnp.dot(patch_latent, w_mesh, preferred_element_type=jnp.float32).astype(
         jnp.bfloat16
@@ -102,26 +319,14 @@
         )
         for corner in range(3)
     ).astype(jnp.bfloat16)
-    node_parts = lax.all_to_all(
-        node_part.reshape(subs, patch_size // subs, width),
-        "sub",
-        split_axis=0,
-        concat_axis=0,
-        tiled=True,
-    )
     grid_part = contract_rows(latent_rows, grid_proj_grad)
     mesh_part = contract_rows(patch_latent, node_part)
     parts = jnp.concatenate([mesh_part, grid_part, msg_part, out_part], axis=1).astype(jnp.bfloat16)
-    exchanged = lax.all_to_all(
+    totals, mesh_proj_grad = reduce_all(
         parts.reshape(devices, width // devices, parts.shape[1]),
-        both,
-        split_axis=0,
-        concat_axis=0,
-        tiled=True,
-    )
-    own_rows = jnp.sum(exchanged.astype(jnp.float32), axis=0).astype(jnp.bfloat16)
-    totals = lax.all_gather(own_rows, both, axis=0, tiled=True)
-    mesh_proj_grad = jnp.sum(node_parts.astype(jnp.float32), axis=0).astype(jnp.bfloat16)
+        node_part.reshape(subs, patch_size // subs, width),
+    )
+    totals = totals.reshape(parts.shape)
     mesh_grad = times_transpose(mesh_proj_grad, w_mesh).astype(jnp.bfloat16)
     grad_scale = 1.0 / math.sqrt(3.0 * total_points)
     scaled = totals.astype(jnp.float32) * grad_scale
@@ -130,7 +335,7 @@
         scaled[:, :width],
         scaled[:, width : 2 * width],
         scaled[:, 2 * width : 3 * width],
-        scaled[:, 3 * width :],
+        scaled[:, 3 * width : 3 * width + channels],
     )
 
 

time: 263 us -> 221 us (0.84)
  the two profiles are of different devices: /device:TPU:0 before, /device:TPU:31 now
where the time goes in v2:
time: 221 us; the launch traced here: 220 us
  waiting for transfers between devices  70.4 us (32%)
  Pallas kernels  57.4 us (26%)
  matrix products  52.9 us (24%)
  between operations  14.3 us (6%)
  starting transfers between devices  12.1 us (5%)
  local copies, waits for them, and re-layouts  8.27 us (4%)
  other arithmetic  4.52 us (2%)
    pallas_call x1, Pallas kernels, reduce_all(): pl.pallas_call(functools.partial(reduce_kernel, subs), out_shape=(jax.Sha...  57.4 us
    all_gather x1, waiting for transfers between devices, shards(): patch_latent = lax.all_gather(mesh_latent, 'sub', axis=0, tiled=True)  28.8 us
    all_to_all x1, waiting for transfers between devices, shards(): lax.all_to_all(grad_send.reshape(devices, capacity, channels + padding),...  23.3 us
    all_to_all x1, waiting for transfers between devices, shards(): lax.all_to_all(latent_send.reshape(devices, capacity, width), both, split...  17.7 us
    dot_general x4, matrix products, times_transpose(): lax.dot_general(left, right, (((1,), (1,)), ((), ())), preferred_element_...  14.9 us
    dot_general x3, matrix products, shards(): jnp.dot((nodes == local_node[corner][:, None]).astype(jnp.bfloat16), patc...  12.3 us
    dot_general x3, matrix products, shards(): jnp.dot((targets == local_node[corner][None, :]).astype(jnp.bfloat16), pr...  9.98 us
    all_to_all x1, starting transfers between devices, shards(): lax.all_to_all(grad_send.reshape(devices, capacity, channels + padding),...  6.13 us
  transfers between devices with their start and end apart: 3, of which 3 were waited for; matrix products, arithmetic and copies ran while one was open for 4% of the time, Pallas kernels for 0%

profile of v2, /device:TPU:31, one launch (start us, length us, event | category | flops | bytes accessed | tf_op | source)
XLA Modules:
  0.0 220.0 jit_solution(5132698329173245291)
XLA Ops:
  8.4 3.2 %fusion.15 = bf16[2304,256]{1,0:T(8,128)(2,1)} fusion(s32[768]{0:T(1024)} %param.12, bf16[227,768]{1,0:T(8,128)(2,1)S(1)} %multiply_convert_fusion.3), kind=kOutput, calls=%fused_computation.36 | convolution fusion | flops 908328960 | bytes 1531392 | tf_op jit(solution)/shard_map/dot_general | solution.py:29
  11.5 6.1 %all-to-all-start = ((bf16[32,72,256]{2,1,0:T(8,128)(2,1)}), bf16[32,72,256]{2,1,0:T(8,128)(2,1)S(1)}, u32[]{:S(2)}, u32[]{:S(2)}) async-start(bf16[32,72,256]{2,1,0:T(8,128)(2,1)} %bitcast), calls=%async_computation | async-start | bytes 2359296 | tf_op jit(solution)/shard_map/all_to_all | solution.py:272
  17.7 3.4 %fusion.14 = bf16[2304,512]{1,0:T(8,128)(2,1)} fusion(bf16[768,512]{1,0:T(8,128)(2,1)S(1)} %copy-done, s32[768]{0:T(1024)S(1)} %copy-done.12), kind=kOutput, calls=%fused_computation.32 | convolution fusion | flops 1814888448 | bytes 3148800 | tf_op jit(solution)/shard_map/dot_general | solution.py:261
  21.1 23.3 %all-to-all-done = bf16[32,72,256]{2,1,0:T(8,128)(2,1)S(1)} async-done(((bf16[32,72,256]{2,1,0:T(8,128)(2,1)}), bf16[32,72,256]{2,1,0:T(8,128)(2,1)S(1)}, u32[]{:S(2)}, u32[]{:S(2)}) %all-to-all-start) | async-done | bytes 1179680 | tf_op jit(solution)/shard_map/all_to_all | solution.py:272
  44.4 5.9 %all-to-all-start.1 = ((bf16[32,72,512]{2,1,0:T(8,128)(2,1)}), bf16[32,72,512]{2,1,0:T(8,128)(2,1)}, u32[]{:S(2)}, u32[]{:S(2)}) async-start(bf16[32,72,512]{2,1,0:T(8,128)(2,1)} %bitcast.52), calls=%async_computation.1 | async-start | bytes 4718592 | tf_op jit(solution)/shard_map/all_to_all | solution.py:265
  51.2 28.8 %all-gather.2.cloned.1.call-done = bf16[1280,512]{1,0:T(8,128)(2,1)} async-done(((bf16[320,512]{1,0:T(8,128)(2,1)}), bf16[1280,512]{1,0:T(8,128)(2,1)}) %all-gather.2.cloned.1.call-update) | async-done | bytes 1310736 | tf_op jit(solution)/shard_map/all_gather | solution.py:259
  80.0 3.2 %convolution_convert_fusion.3 = bf16[1280,512]{1,0:T(8,128)(2,1)} fusion(bf16[1280,512]{1,0:T(8,128)(2,1)} %all-gather.2.cloned.1.call-done, bf16[512,512]{1,0:T(8,128)(2,1)S(1)} %copy-done.4), kind=kOutput, calls=%fused_computation.42 | convolution fusion | flops 671744000 | bytes 3145728 | tf_op jit(solution)/shard_map/dot_general | solution.py:280
  83.3 2.2 %convolution_convert_fusion.2 = bf16[2304,512]{1,0:T(8,128)(2,1)} fusion(bf16[2304,256]{1,0:T(8,128)(2,1)S(1)} %bitcast.50, bf16[512,227]{0,1:T(8,128)(2,1)S(1)} %copy-done.7), kind=kOutput, calls=%fused_computation.35 | convolution fusion | flops 605159424 | bytes 3771392 | tf_op jit(solution)/shard_map/dot_general | solution.py:29
  85.5 17.7 %all-to-all-done.1 = bf16[32,72,512]{2,1,0:T(8,128)(2,1)} async-done(((bf16[32,72,512]{2,1,0:T(8,128)(2,1)}), bf16[32,72,512]{2,1,0:T(8,128)(2,1)}, u32[]{:S(2)}, u32[]{:S(2)}) %all-to-all-start.1) | async-done | bytes 2359328 | tf_op jit(solution)/shard_map/all_to_all | solution.py:265
  103.1 4.3 %copy.14 = bf16[2304,512]{0,1:T(8,128)(2,1)} copy(bf16[2304,512]{1,0:T(8,128)(2,1)} %bitcast.3) | data formatting | bytes 4718592 | tf_op jit(solution)/shard_map/reshape | solution.py:271
  107.5 3.1 %convolution_convert_fusion.1 = bf16[2304,512]{1,0:T(8,128)(2,1)S(1)} fusion(bf16[2304,512]{1,0:T(8,128)(2,1)} %bitcast.3, bf16[512,512]{1,0:T(8,128)(2,1)S(1)} %copy-done.10), kind=kOutput, calls=%fused_computation.34 | convolution fusion | flops 1209139200 | bytes 5242880 | tf_op jit(solution)/shard_map/dot_general | solution.py:286
  110.6 3.5 %convert_add_fusion.1 = f32[2304,512]{1,0:T(8,128)S(1)} fusion(bf16[2304,512]{1,0:T(8,128)(2,1)S(1)} %convolution_convert_fusion.1, bf16[1280,512]{1,0:T(8,128)(2,1)S(1)} %copy-done.13, s32[2304]{0:T(1024)S(1)} %get-tuple-element.11), kind=kOutput, calls=%fused_computation.16 | convolution fusion | flops 3025207296 | bytes 8397824 | tf_op jit(solution)/shard_map/dot_general | solution.py:291
  114.1 3.5 %convert_add_fusion = f32[2304,512]{1,0:T(8,128)S(1)} fusion(bf16[2304,512]{1,0:T(8,128)(2,1)S(1)} %convolution_convert_fusion.1, bf16[1280,512]{1,0:T(8,128)(2,1)S(1)} %copy-done.13, s32[2304]{0:T(1024)S(1)} %get-tuple-element.10), kind=kOutput, calls=%fused_computation.15 | convolution fusion | flops 3025207296 | bytes 8397824 | tf_op jit(solution)/shard_map/dot_general | solution.py:291
  117.6 5.3 %convert_add_fusion.2 = f32[2304,512]{1,0:T(8,128)} fusion(bf16[2304,512]{1,0:T(8,128)(2,1)S(1)} %convolution_convert_fusion.1, bf16[1280,512]{1,0:T(8,128)(2,1)S(1)} %copy-done.13, s32[2304]{0:T(1024)S(1)} %get-tuple-element.9), kind=kOutput, calls=%fused_computation.17 | convolution fusion | flops 3025207296 | bytes 8397824 | tf_op jit(solution)/shard_map/dot_general | solution.py:291
  122.9 8.4 %multiply_convert_fusion.2 = (bf16[2304,512]{1,0:T(8,128)(2,1)S(1)}, bf16[2304,512]{1,0:T(8,128)(2,1)S(1)}, bf16[2304,512]{1,0:T(8,128)(2,1)S(1)}, bf16[2304,512]{1,0:T(8,128)(2,1)S(1)}) fusion(f32[2304,512]{1,0:T(8,128)} %convert_add_fusion.2, f32[2304,512]{1,0:T(8,128)S(1)} %convert_add_fusion, f32[2304,512]{1,0:T(8,128)S(1)} %convert_add_fusion.1, ...), kind=kOutput, calls=%fused_computation.30 | convolution fusion | flops 1246887936 | bytes 26476544 | tf_op jit(solution)/shard_map/dot_general | solution.py:29
  131.3 1.4 convolution_convert_fusion.5
  132.8 1.4 convolution_convert_fusion
  134.2 3.2 %fusion = f32[1280,512]{1,0:T(8,128)S(1)} fusion(bf16[2304,512]{1,0:T(8,128)(2,1)S(1)} %get-tuple-element.12, s32[2304]{0:T(1024)S(1)} %get-tuple-element.9), kind=kOutput, calls=%fused_computation.6 | convolution fusion | flops 3022848000 | bytes 4989952 | tf_op jit(solution)/shard_map/dot_general | solution.py:315
  137.4 3.2 %fusion.19 = f32[1280,512]{1,0:T(8,128)S(1)} fusion(f32[1280,512]{1,0:T(8,128)S(1)} %fusion, bf16[2304,512]{1,0:T(8,128)(2,1)S(1)} %get-tuple-element.15, s32[2304]{0:T(1024)S(1)} %get-tuple-element.11), kind=kOutput, calls=%fused_computation.41 | convolution fusion | flops 3023503360 | bytes 7611392 | tf_op jit(solution)/shard_map/dot_general | solution.py:315
  140.7 1.5 fusion.24
  142.2 3.5 %fusion.20 = bf16[1280,512]{1,0:T(8,128)(2,1)S(1)} fusion(f32[1280,512]{1,0:T(8,128)S(1)} %fusion.19, bf16[2304,512]{1,0:T(8,128)(2,1)S(1)} %get-tuple-element.14, s32[2304]{0:T(1024)S(1)} %get-tuple-element.10), kind=kOutput, calls=%fused_computation.43 | convolution fusion | flops 3024158720 | bytes 6300672 | tf_op jit(solution)/shard_map/dot_general | solution.py:315
  149.8 57.4 %shard_map.128 = (bf16[32,16,1792]{2,1,0:T(8,128)(2,1)}, bf16[320,512]{1,0:T(8,128)(2,1)}) custom-call(bf16[32,16,1792]{2,1,0:T(8,128)(2,1)} %pad_maximum_fusion.parts_ref, bf16[4,320,512]{2,1,0:T(8,128)(2,1)} %bitcast.54), custom_call_target="tpu_custom_call" | custom-call | tf_op jit(solution)/shard_map/pallas_call | solution.py:225
  207.3 2.0 convert_multiply_fusion
  209.3 1.8 fusion.31
  (40 shorter events, 8.2 us)
Async XLA Ops:
  7.2 10.5 %copy-start = (bf16[768,512]{1,0:T(8,128)(2,1)S(1)}, bf16[768,512]{1,0:T(8,128)(2,1)}, u32[]{:S(2)}) copy-start(bf16[768,512]{1,0:T(8,128)(2,1)} %param.10) | copy-start | bytes 2359300
  8.3 9.3 %copy-start.12 = (s32[768]{0:T(1024)S(1)}, s32[768]{0:T(1024)}, u32[]{:S(2)}) copy-start(s32[768]{0:T(1024)} %param.12) | copy-start | bytes 9220
  11.5 32.9 %all-to-all-start = ((bf16[32,72,256]{2,1,0:T(8,128)(2,1)}), bf16[32,72,256]{2,1,0:T(8,128)(2,1)S(1)}, u32[]{:S(2)}, u32[]{:S(2)}) async-start(bf16[32,72,256]{2,1,0:T(8,128)(2,1)} %bitcast), calls=%async_computation | async-start | bytes 2359296 | tf_op jit(solution)/shard_map/all_to_all | solution.py:272
  21.1 30.0 %copy-start.8 = (s32[3,2304]{1,0:T(4,128)S(1)}, s32[3,2304]{1,0:T(4,128)}, u32[]{:S(2)}) copy-start(s32[3,2304]{1,0:T(4,128)} %param.13) | copy-start | bytes 82948
  21.1 58.9 %copy-start.4 = (bf16[512,512]{1,0:T(8,128)(2,1)S(1)}, bf16[512,512]{1,0:T(8,128)(2,1)}, u32[]{:S(2)}) copy-start(bf16[512,512]{1,0:T(8,128)(2,1)} %param.14) | copy-start | bytes 1572868
  44.4 58.7 %all-to-all-start.1 = ((bf16[32,72,512]{2,1,0:T(8,128)(2,1)}), bf16[32,72,512]{2,1,0:T(8,128)(2,1)}, u32[]{:S(2)}, u32[]{:S(2)}) async-start(bf16[32,72,512]{2,1,0:T(8,128)(2,1)} %bitcast.52), calls=%async_computation.1 | async-start | bytes 4718592 | tf_op jit(solution)/shard_map/all_to_all | solution.py:265
  50.4 32.9 %copy-start.7 = (bf16[512,227]{0,1:T(8,128)(2,1)S(1)}, bf16[512,227]{0,1:T(8,128)(2,1)}, u32[]{:S(2)}) copy-start(bf16[512,227]{0,1:T(8,128)(2,1)} %param.17) | copy-start | bytes 697348
  50.4 29.7 %all-gather.2.cloned.1.call-start = ((), (), s32[]{:S(2)}) async-start(), calls=%async_computation.2 | async-start | bytes 1638400 | tf_op jit(solution)/shard_map/all_gather | solution.py:259
  85.5 22.0 %copy-start.10 = (bf16[512,512]{1,0:T(8,128)(2,1)S(1)}, bf16[512,512]{1,0:T(8,128)(2,1)}, u32[]{:S(2)}) copy-start(bf16[512,512]{1,0:T(8,128)(2,1)} %param.15) | copy-start | bytes 1572868
  107.4 3.2 %copy-start.13 = (bf16[1280,512]{1,0:T(8,128)(2,1)S(1)}, bf16[1280,512]{1,0:T(8,128)(2,1)}, u32[]{:S(2)}) copy-start(bf16[1280,512]{1,0:T(8,128)(2,1)} %convolution_convert_fusion.3) | copy-start | bytes 3932164
  117.6 5.4 %copy-start.1 = (bf16[2304,512]{1,0:T(8,128)(2,1)S(1)}, bf16[2304,512]{1,0:T(8,128)(2,1)}, u32[]{:S(2)}) copy-start(bf16[2304,512]{1,0:T(8,128)(2,1)} %convolution_convert_fusion.2) | copy-start | bytes 7077892
  117.6 5.4 %copy-start.11 = (bf16[512,512]{1,0:T(8,128)(2,1)S(1)}, bf16[512,512]{1,0:T(8,128)(2,1)}, u32[]{:S(2)}) copy-start(bf16[512,512]{1,0:T(8,128)(2,1)} %param.16) | copy-start | bytes 1572868
  137.4 3.3 %copy-start.2 = (bf16[2304,512]{0,1:T(8,128)(2,1)S(1)}, bf16[2304,512]{0,1:T(8,128)(2,1)}, u32[]{:S(2)}) copy-start(bf16[2304,512]{0,1:T(8,128)(2,1)} %copy.14) | copy-start | bytes 7077892
  145.7 2.7 %copy-start.3 = (bf16[1280,512]{1,0:T(8,128)(2,1)}, bf16[1280,512]{1,0:T(8,128)(2,1)S(1)}, u32[]{:S(2)}) copy-start(bf16[1280,512]{1,0:T(8,128)(2,1)S(1)} %fusion.20) | copy-start | bytes 3932164
  145.8 1.8 copy-start.9
  209.3 1.8 copy-start.5
  209.3 1.8 copy-start.6
Sparse Core Ops, SparseCore 0:
  52.7 27.2 all-gather.1
